TPU v7x, 32 devices: a whole 2x2x4 slice. The times are simulated.
32 devices in a mesh: blk: 8 (over y, x, core), rep: 4 (over z).
Axes of the slice: x: 2, y: 2, z: 4, core: 2. Of those that a mesh axis runs over, the one named last changes fastest.
Arguments:
- image: bfloat16 [4096, 1024], P(('blk', 'rep')), may hold values from -100 to 100
- text: bfloat16 [4096, 1024], P(('blk', 'rep')), may hold values from -100 to 100
- positive: int32 [8, 512], P('blk', 'rep'), may hold values from 0 to 511, each once within a row
- logit_scale: float32 [1], replicated, may hold values from 85 to 270
Outputs:
- row_loss: float32 [4096], P(('blk', 'rep'))
- col_loss: float32 [4096], P(('blk', 'rep'))
- img_grad: float32 [4096, 1024], P(('blk', 'rep'))
- txt_grad: float32 [4096, 1024], P(('blk', 'rep'))
Inputs may be any that keep to these rules, and one draw needn't show every extreme that they name: Each row of positive names every index of its block once.
All inputs are finite; a program needn't handle non-finite values.
Results may differ from a plain program's by a relative error of at most 0.0081.
The roundings to bfloat16 on the way count: a program that leaves them out, or rounds other values in their place, can miss the bound.
Values may be sent and summed in bfloat16 or wider, within the bound.
No kernel may reach another device: no remote copies, remote signals or barrier semaphores. Data moves between devices by JAX's collectives and lax.ppermute only.
A program may use at most 64 MiB of HBM per device.

v0:
```python
import jax
import jax.numpy as jnp
from jax import lax
from jax.sharding import PartitionSpec as P

STEPS = 4


def passed_along(array, axis, by):
    count = lax.axis_size(axis)
    return lax.ppermute(array, axis, [(i, (i + by) % count) for i in range(count)])


def combined_all(part, axis, combine):
    gathered = jax.tree.map(lambda a: lax.all_gather(a, axis), part)

    def take(source):
        return jax.tree.map(lambda a: lax.dynamic_index_in_dim(a, source, 0, False), gathered)

    return lax.fori_loop(
        1, lax.axis_size(axis), lambda source, state: combine(state, take(source)), take(0)
    )


def normalize(values):
    widened = values.astype(jnp.float32)
    inverse = lax.rsqrt(jnp.sum(widened * widened, axis=-1, keepdims=True) + 1e-06)
    return (widened * inverse, inverse)


def combine_stats(earlier, later):
    highest = jnp.maximum(earlier[0], later[0])
    summed = earlier[1] * jnp.exp(earlier[0] - highest) + later[1] * jnp.exp(later[0] - highest)
    return (highest, summed, earlier[2] + later[2])


def tile_scores(img_part, text_tile, factor):
    return factor * jnp.einsum("id,jd->ij", img_part, text_tile, preferred_element_type=jnp.float32)


def tile_weights(img_part, text_tile, factor, row_lse, col_lse, onehot):
    scores = tile_scores(img_part, text_tile, factor)
    weight = 0.5 * (jnp.exp(scores - row_lse[:, None]) + jnp.exp(scores - col_lse[None, :]))
    if onehot is not None:
        weight = weight - onehot
    return weight.astype(jnp.bfloat16)


def on_device(image, text, positive, logit_scale):
    factor = logit_scale[0]
    row_count = image.shape[0]
    width = image.shape[1]
    quarter = lax.axis_index("rep")
    img_unit, img_inverse = normalize(image)
    txt_unit, txt_inverse = normalize(text)
    img_tile = img_unit.astype(jnp.bfloat16)
    txt_own = txt_unit.astype(jnp.bfloat16)
    home_tile = lax.all_gather(txt_own, "rep", axis=0, tiled=True)
    block_rows = home_tile.shape[0]
    columns = lax.broadcasted_iota(jnp.int32, (row_count, block_rows), 1)
    onehot = (positive[0][:, None] == columns).astype(jnp.float32)
    kept = []
    moving = img_tile
    for loop_step in range(STEPS):
        if loop_step > 0:
            moving = passed_along(moving, "blk", -1)
            row_max, row_sum = passed_along((row_max, row_sum), "blk", -1)
        kept.append(moving)
        scores = tile_scores(moving, home_tile, factor)
        row_peak = jnp.max(scores, axis=1)
        col_peak = jnp.max(scores, axis=0)
        col_part = jnp.sum(jnp.exp(scores - col_peak[None, :]), axis=0)
        if loop_step == 0:
            row_max = row_peak
            row_sum = jnp.sum(jnp.exp(scores - row_peak[:, None]), axis=1)
            row_pos = jnp.sum(onehot * scores, axis=1)
            col_max, col_sum, col_pos = (col_peak, col_part, jnp.sum(onehot * scores, axis=0))
        else:
            highest = jnp.maximum(row_max, row_peak)
            row_sum = row_sum * jnp.exp(row_max - highest) + jnp.sum(
                jnp.exp(scores - highest[:, None]), axis=1
            )
            row_max = highest
            col_max, col_sum, col_pos = combine_stats(
                (col_max, col_sum, col_pos), (col_peak, col_part, jnp.zeros_like(col_peak))
            )
    col_max, col_sum, col_pos = combined_all((col_max, col_sum, col_pos), "rep", combine_stats)
    col_lse = col_max + jnp.log(col_sum)
    row_lse = row_max + jnp.log(row_sum)
    travel = (row_lse, jnp.zeros((row_count, width), jnp.float32))
    text_terms = jnp.zeros((block_rows, width), jnp.float32)
    for loop_step in range(STEPS - 1, -1, -1):
        if loop_step < STEPS - 1:
            travel = passed_along((travel[0], travel[1]), "blk", 1)
        tile = kept[loop_step]
        weight = tile_weights(
            tile, home_tile, factor, travel[0], col_lse, onehot if loop_step == 0 else None
        )
        travel = (
            travel[0],
            travel[1] + jnp.dot(weight, home_tile, preferred_element_type=jnp.float32),
        )
        text_terms = text_terms + jnp.einsum(
            "ij,id->jd", weight, tile, preferred_element_type=jnp.float32
        )
    row_lse, img_acc = travel
    col_lse_home, col_pos_home = (col_lse, col_pos)
    row_loss = row_lse - row_pos
    text_share = lax.psum_scatter(text_terms, "rep", scatter_dimension=0, tiled=True)
    img_sum = factor * img_acc
    txt_sum = factor * text_share
    img_grad = (
        img_sum - img_unit * jnp.sum(img_unit * img_sum, axis=-1, keepdims=True)
    ) * img_inverse
    txt_grad = (
        txt_sum - txt_unit * jnp.sum(txt_unit * txt_sum, axis=-1, keepdims=True)
    ) * txt_inverse
    col_whole = col_lse_home - col_pos_home
    col_loss = lax.dynamic_slice_in_dim(col_whole, quarter * row_count, row_count)
    return (row_loss, col_loss, img_grad, txt_grad)


def solution(mesh):
    placed = (P(("blk", "rep"), None), P(("blk", "rep"), None), P("blk", "rep"), P())
    return jax.shard_map(
        on_device,
        mesh=mesh,
        in_specs=placed,
        out_specs=(
            P(("blk", "rep")),
            P(("blk", "rep")),
            P(("blk", "rep"), None),
            P(("blk", "rep"), None),
        ),
        check_vma=False,
    )
```

profile of v0, /device:TPU:0, one launch (start us, length us, event | category | flops | bytes accessed | tf_op | source)
XLA Modules:
  0.0 154.7 jit_solution(10748212426085432188)
XLA Ops:
  7.2 1.1 fusion.13
  8.3 1.8 %fusion.2 = bf16[128,1024]{1,0:T(8,128)(2,1)} fusion(bf16[128,1024]{1,0:T(8,128)(2,1)} %param.7, f32[128]{0:T(128)S(1)} %add_rsqrt_fusion), kind=kLoop, calls=%fused_computation.14 | loop fusion | flops 393216 | bytes 524800 | tf_op jit(solution)/shard_map/convert_element_type | solution.py:57
  10.2 1.1 fusion.9
  11.2 1.1 fusion.5
  12.3 3.4 %collective-permute-start.1 = (bf16[128,1024]{1,0:T(8,128)(2,1)S(1)}, bf16[128,1024]{1,0:T(8,128)(2,1)S(1)}, u32[]{:S(2)}, u32[]{:S(2)}) collective-permute-start(bf16[128,1024]{1,0:T(8,128)(2,1)S(1)} %fusion.5), channel_id=1, source_target_pairs={{0,28},{4,0},{8,4},{12,8},{16,12},{20,16},{24,20},{28,24},{1,29},{... | collective-permute-start | bytes 786440 | tf_op jit(solution)/shard_map/ppermute | solution.py:11
  15.7 3.9 %collective-permute-done.1 = bf16[128,1024]{1,0:T(8,128)(2,1)S(1)} collective-permute-done((bf16[128,1024]{1,0:T(8,128)(2,1)S(1)}, bf16[128,1024]{1,0:T(8,128)(2,1)S(1)}, u32[]{:S(2)}, u32[]{:S(2)}) %collective-permute-start.1) | collective-permute-done | bytes 262176 | tf_op jit(solution)/shard_map/ppermute | solution.py:11
  19.6 2.8 %collective-permute-start.3 = (bf16[128,1024]{1,0:T(8,128)(2,1)S(1)}, bf16[128,1024]{1,0:T(8,128)(2,1)S(1)}, u32[]{:S(2)}, u32[]{:S(2)}) collective-permute-start(bf16[128,1024]{1,0:T(8,128)(2,1)S(1)} %collective-permute-done.1), channel_id=1, source_target_pairs={{0,28},{4,0},{8,4},{12,8},{16,12},{20,16},{24,20},{28,24},{1,29},{... | collective-permute-start | bytes 786440 | tf_op jit(solution)/shard_map/ppermute | solution.py:11
  23.1 3.2 %collective-permute-done.3 = bf16[128,1024]{1,0:T(8,128)(2,1)S(1)} collective-permute-done((bf16[128,1024]{1,0:T(8,128)(2,1)S(1)}, bf16[128,1024]{1,0:T(8,128)(2,1)S(1)}, u32[]{:S(2)}, u32[]{:S(2)}) %collective-permute-start.3) | collective-permute-done | bytes 262176 | tf_op jit(solution)/shard_map/ppermute | solution.py:11
  26.3 3.2 %collective-permute-start.5 = (bf16[128,1024]{1,0:T(8,128)(2,1)S(1)}, bf16[128,1024]{1,0:T(8,128)(2,1)S(1)}, u32[]{:S(2)}, u32[]{:S(2)}) collective-permute-start(bf16[128,1024]{1,0:T(8,128)(2,1)S(1)} %collective-permute-done.3), channel_id=1, source_target_pairs={{0,28},{4,0},{8,4},{12,8},{16,12},{20,16},{24,20},{28,24},{1,29},{... | collective-permute-start | bytes 786440 | tf_op jit(solution)/shard_map/ppermute | solution.py:11
  29.5 11.4 %all-gather.6.cloned.1.call-done = bf16[512,1024]{1,0:T(8,128)(2,1)} async-done(((bf16[128,1024]{1,0:T(8,128)(2,1)}), bf16[512,1024]{1,0:T(8,128)(2,1)}) %all-gather.6.cloned.1.call-update) | async-done | bytes 1048592 | tf_op jit(solution)/shard_map/all_gather | solution.py:58
  41.0 1.9 %fusion.25 = (f32[512]{0:T(512)S(1)}, f32[128]{0:T(128)S(1)}, f32[128,512]{1,0:T(8,128)S(1)}) fusion(bf16[128,1024]{1,0:T(8,128)(2,1)S(1)} %fusion.5, bf16[512,1024]{1,0:T(8,128)(2,1)} %all-gather.6.cloned.1.call-done, f32[]{:T(128)} %bitcast.52), kind=kOutput, calls=%fused_computation.64 | convolution fusion | flops 134413696 | bytes 1575428 | tf_op jit(solution)/shard_map/id,jd->ij/dot_general | solution.py:38
  42.9 0.2 fusion.15
  43.1 11.9 %all-gather.3 = f32[4,1,512]{2,1,0:T(1,128)S(1)} all-gather(f32[1,1,512]{2,1,0:T(1,128)S(1)} %bitcast.77), channel_id=2, replica_groups=mesh['blk'=8,'rep'=4] {'rep'}, dimensions={0}, use_global_device_ids=true | all-gather | bytes 10240 | tf_op jit(solution)/shard_map/all_gather | solution.py:15
  55.1 2.5 %collective-permute-start.6 = (f32[128]{0:T(128)S(1)}, f32[128]{0:T(128)S(1)}, u32[]{:S(2)}, u32[]{:S(2)}) collective-permute-start(f32[128]{0:T(128)S(1)} %get-tuple-element.188), channel_id=1, source_target_pairs={{0,28},{4,0},{8,4},{12,8},{16,12},{20,16},{24,20},{28,24},{1,29},{... | collective-permute-start | bytes 1544 | tf_op jit(solution)/shard_map/ppermute | solution.py:11
  57.6 0.6 fusion.24
  58.1 0.6 fusion.26
  58.7 0.6 fusion.27
  59.3 0.1 collective-permute-start.2
  59.4 0.2 exponential_reduce_fusion.2
  59.6 1.8 %collective-permute-start.7 = (f32[128]{0:T(128)S(1)}, f32[128]{0:T(128)S(1)}, u32[]{:S(2)}, u32[]{:S(2)}) collective-permute-start(f32[128]{0:T(128)S(1)} %multiply_add_fusion.2), channel_id=1, source_target_pairs={{0,28},{4,0},{8,4},{12,8},{16,12},{20,16},{24,20},{28,24},{1,29},{... | collective-permute-start | bytes 1544 | tf_op jit(solution)/shard_map/ppermute | solution.py:11
  61.5 1.8 %collective-permute-start.4 = (f32[128]{0:T(128)S(1)}, f32[128]{0:T(128)S(1)}, u32[]{:S(2)}, u32[]{:S(2)}) collective-permute-start(f32[128]{0:T(128)S(1)} %max.62), channel_id=1, source_target_pairs={{0,28},{4,0},{8,4},{12,8},{16,12},{20,16},{24,20},{28,24},{1,29},{... | collective-permute-start | bytes 1544 | tf_op jit(solution)/shard_map/ppermute | solution.py:11
  63.3 0.2 exponential_reduce_fusion.1
  63.5 1.8 %collective-permute-start.8 = (f32[128]{0:T(128)S(1)}, f32[128]{0:T(128)S(1)}, u32[]{:S(2)}, u32[]{:S(2)}) collective-permute-start(f32[128]{0:T(128)S(1)} %multiply_add_fusion.1), channel_id=1, source_target_pairs={{0,28},{4,0},{8,4},{12,8},{16,12},{20,16},{24,20},{28,24},{1,29},{... | collective-permute-start | bytes 1544 | tf_op jit(solution)/shard_map/ppermute | solution.py:11
  65.4 0.2 exponential_reduce_fusion
  65.6 11.9 %all-gather.2 = f32[4,1,512]{2,1,0:T(1,128)S(1)} all-gather(f32[1,1,512]{2,1,0:T(1,128)S(1)} %get-tuple-element.223), channel_id=1, replica_groups=mesh['blk'=8,'rep'=4] {'rep'}, dimensions={0}, use_global_device_ids=true | all-gather | bytes 10240 | tf_op jit(solution)/shard_map/all_gather | solution.py:15
  77.6 11.9 %all-gather.1 = f32[4,1,512]{2,1,0:T(1,128)S(1)} all-gather(f32[1,1,512]{2,1,0:T(1,128)S(1)} %get-tuple-element.224), channel_id=1, replica_groups=mesh['blk'=8,'rep'=4] {'rep'}, dimensions={0}, use_global_device_ids=true | all-gather | bytes 10240 | tf_op jit(solution)/shard_map/all_gather | solution.py:15
  89.5 0.3 while.19
  89.8 0.1 collective-permute-start.9
  89.9 3.9 %collective-permute-done.9 = f32[128]{0:T(128)S(1)} collective-permute-done((f32[128]{0:T(128)S(1)}, f32[128]{0:T(128)S(1)}, u32[]{:S(2)}, u32[]{:S(2)}) %collective-permute-start.9) | collective-permute-done | bytes 544 | tf_op jit(solution)/shard_map/ppermute | solution.py:11
  93.7 0.5 fusion.18
  94.3 3.4 %collective-permute-done.10 = f32[128]{0:T(128)S(1)} collective-permute-done((f32[128]{0:T(128)S(1)}, f32[128]{0:T(128)S(1)}, u32[]{:S(2)}, u32[]{:S(2)}) %collective-permute-start.10) | collective-permute-done | bytes 544 | tf_op jit(solution)/shard_map/ppermute | solution.py:11
  97.6 0.5 fusion.19
  98.2 3.3 %collective-permute-done.11 = f32[128]{0:T(128)S(1)} collective-permute-done((f32[128]{0:T(128)S(1)}, f32[128]{0:T(128)S(1)}, u32[]{:S(2)}, u32[]{:S(2)}) %collective-permute-start.11) | collective-permute-done | bytes 544 | tf_op jit(solution)/shard_map/ppermute | solution.py:11
  101.5 0.6 fusion.22
  102.1 1.9 %add_add_fusion = f32[512,1024]{1,0:T(8,128)} fusion(f32[512,1024]{1,0:T(8,128)S(1)} %fusion.22, f32[512,1024]{1,0:T(8,128)S(1)} %fusion.19, f32[512,1024]{1,0:T(8,128)S(1)} %fusion.18, bf16[128,1024]{1,0:T(8,128)(2,1)S(1)} %collective-permute-done.5, f32[128,512]{1,0:T(8,128)S(1)} %get-tuple-element.228, f32[512]{0:T(512)S(1)} %get-tuple-element.220, ...), kind=kOutput, calls=%fused_computation.4 | convolution fusion | flops 136118272 | bytes 8915456 | tf_op jit(solution)/shard_map/ij,id->jd/dot_general | solution.py:103
  104.0 0.4 fusion.17
  104.5 9.5 %collective-permute-done.12 = f32[128,1024]{1,0:T(8,128)S(1)} collective-permute-done((f32[128,1024]{1,0:T(8,128)S(1)}, f32[128,1024]{1,0:T(8,128)S(1)}, u32[]{:S(2)}, u32[]{:S(2)}) %collective-permute-start.12) | collective-permute-done | bytes 524320 | tf_op jit(solution)/shard_map/ppermute | solution.py:11
  114.0 0.4 convolution_add_fusion
  114.4 9.5 %collective-permute-done.13 = f32[128,1024]{1,0:T(8,128)S(1)} collective-permute-done((f32[128,1024]{1,0:T(8,128)S(1)}, f32[128,1024]{1,0:T(8,128)S(1)}, u32[]{:S(2)}, u32[]{:S(2)}) %collective-permute-start.13) | collective-permute-done | bytes 524320 | tf_op jit(solution)/shard_map/ppermute | solution.py:11
  123.9 0.4 fusion.21
  124.4 0.6 dynamic_slice.46
  124.9 0.5 sub.237
  125.5 8.4 %collective-permute-done.14 = f32[128,1024]{1,0:T(8,128)S(1)} collective-permute-done((f32[128,1024]{1,0:T(8,128)S(1)}, f32[128,1024]{1,0:T(8,128)S(1)}, u32[]{:S(2)}, u32[]{:S(2)}) %collective-permute-start.14) | collective-permute-done | bytes 524320 | tf_op jit(solution)/shard_map/ppermute | solution.py:11
  133.9 0.5 fusion.6
  134.3 1.0 fusion.8
  135.4 9.2 %reduce-scatter.2.cloned.1.call-done = f32[128,1024]{1,0:T(8,128)} async-done(((f32[512,1024]{1,0:T(8,128)}), f32[128,1024]{1,0:T(8,128)}) %reduce-scatter.2.cloned.1.call-update) | async-done | bytes 524304 | tf_op jit(solution)/shard_map/reduce_scatter | solution.py:109
  144.5 1.3 fusion.10
  145.8 2.1 %fusion.12 = f32[128,1024]{1,0:T(8,128)} fusion(bf16[128,1024]{1,0:T(8,128)(2,1)S(1)} %copy-done.1, f32[128,1024]{1,0:T(8,128)} %reduce-scatter.2.cloned.1.call-done, f32[128]{0:T(128)S(1)} %fusion.10, f32[]{:T(128)} %bitcast.54, f32[128]{0:T(128)S(1)} %add_rsqrt_fusion), kind=kLoop, calls=%fused_computation.26 | loop fusion | flops 786432 | bytes 1311748 | tf_op jit(solution)/shard_map/mul | solution.py:115
  (53 shorter events, 0.6 us)
Async XLA Ops:
  7.2 35.7 %copy-start.3 = (s32[1,128]{1,0:T(1,128)S(1)}, s32[1,128]{1,0:T(1,128)}, u32[]{:S(2)}) copy-start(s32[1,128]{1,0:T(1,128)} %param.8) | copy-start | bytes 1540
  7.2 33.8 %all-gather.6.cloned.1.call-start = ((), (), s32[]{:S(2)}) async-start(), calls=%async_computation.1 | async-start | bytes 1310720 | tf_op jit(solution)/shard_map/all_gather | solution.py:58
  10.1 134.4 %reduce-scatter.2.cloned.1.call-start = ((), (), s32[]{:S(2)}) async-start(), calls=%async_computation.2 | async-start | bytes 2621440 | tf_op jit(solution)/shard_map/reduce_scatter | solution.py:109
  12.3 7.3 %collective-permute-start.1 = (bf16[128,1024]{1,0:T(8,128)(2,1)S(1)}, bf16[128,1024]{1,0:T(8,128)(2,1)S(1)}, u32[]{:S(2)}, u32[]{:S(2)}) collective-permute-start(bf16[128,1024]{1,0:T(8,128)(2,1)S(1)} %fusion.5), channel_id=1, source_target_pairs={{0,28},{4,0},{8,4},{12,8},{16,12},{20,16},{24,20},{28,24},{1,29},{... | collective-permute-start | bytes 786440 | tf_op jit(solution)/shard_map/ppermute | solution.py:11
  19.6 6.7 %collective-permute-start.3 = (bf16[128,1024]{1,0:T(8,128)(2,1)S(1)}, bf16[128,1024]{1,0:T(8,128)(2,1)S(1)}, u32[]{:S(2)}, u32[]{:S(2)}) collective-permute-start(bf16[128,1024]{1,0:T(8,128)(2,1)S(1)} %collective-permute-done.1), channel_id=1, source_target_pairs={{0,28},{4,0},{8,4},{12,8},{16,12},{20,16},{24,20},{28,24},{1,29},{... | collective-permute-start | bytes 786440 | tf_op jit(solution)/shard_map/ppermute | solution.py:11
  26.3 32.4 %collective-permute-start.5 = (bf16[128,1024]{1,0:T(8,128)(2,1)S(1)}, bf16[128,1024]{1,0:T(8,128)(2,1)S(1)}, u32[]{:S(2)}, u32[]{:S(2)}) collective-permute-start(bf16[128,1024]{1,0:T(8,128)(2,1)S(1)} %collective-permute-done.3), channel_id=1, source_target_pairs={{0,28},{4,0},{8,4},{12,8},{16,12},{20,16},{24,20},{28,24},{1,29},{... | collective-permute-start | bytes 786440 | tf_op jit(solution)/shard_map/ppermute | solution.py:11
  41.0 16.6 %copy-start = (bf16[512,1024]{1,0:T(8,128)(2,1)S(1)}, bf16[512,1024]{1,0:T(8,128)(2,1)}, u32[]{:S(2)}) copy-start(bf16[512,1024]{1,0:T(8,128)(2,1)} %all-gather.6.cloned.1.call-done) | copy-start | bytes 3145732
  55.0 4.3 %collective-permute-start = (f32[128]{0:T(128)S(1)}, f32[128]{0:T(128)S(1)}, u32[]{:S(2)}, u32[]{:S(2)}) collective-permute-start(f32[128]{0:T(128)S(1)} %get-tuple-element.198), channel_id=1, source_target_pairs={{0,28},{4,0},{8,4},{12,8},{16,12},{20,16},{24,20},{28,24},{1,29},{... | collective-permute-start | bytes 1544 | tf_op jit(solution)/shard_map/ppermute | solution.py:11
  55.1 4.5 %collective-permute-start.6 = (f32[128]{0:T(128)S(1)}, f32[128]{0:T(128)S(1)}, u32[]{:S(2)}, u32[]{:S(2)}) collective-permute-start(f32[128]{0:T(128)S(1)} %get-tuple-element.188), channel_id=1, source_target_pairs={{0,28},{4,0},{8,4},{12,8},{16,12},{20,16},{24,20},{28,24},{1,29},{... | collective-permute-start | bytes 1544 | tf_op jit(solution)/shard_map/ppermute | solution.py:11
  59.3 2.2 %collective-permute-start.2 = (f32[128]{0:T(128)S(1)}, f32[128]{0:T(128)S(1)}, u32[]{:S(2)}, u32[]{:S(2)}) collective-permute-start(f32[128]{0:T(128)S(1)} %max.61), channel_id=1, source_target_pairs={{0,28},{4,0},{8,4},{12,8},{16,12},{20,16},{24,20},{28,24},{1,29},{... | collective-permute-start | bytes 1544 | tf_op jit(solution)/shard_map/ppermute | solution.py:11
  59.6 3.9 %collective-permute-start.7 = (f32[128]{0:T(128)S(1)}, f32[128]{0:T(128)S(1)}, u32[]{:S(2)}, u32[]{:S(2)}) collective-permute-start(f32[128]{0:T(128)S(1)} %multiply_add_fusion.2), channel_id=1, source_target_pairs={{0,28},{4,0},{8,4},{12,8},{16,12},{20,16},{24,20},{28,24},{1,29},{... | collective-permute-start | bytes 1544 | tf_op jit(solution)/shard_map/ppermute | solution.py:11
  61.5 3.9 %collective-permute-start.4 = (f32[128]{0:T(128)S(1)}, f32[128]{0:T(128)S(1)}, u32[]{:S(2)}, u32[]{:S(2)}) collective-permute-start(f32[128]{0:T(128)S(1)} %max.62), channel_id=1, source_target_pairs={{0,28},{4,0},{8,4},{12,8},{16,12},{20,16},{24,20},{28,24},{1,29},{... | collective-permute-start | bytes 1544 | tf_op jit(solution)/shard_map/ppermute | solution.py:11
  63.5 26.2 %collective-permute-start.8 = (f32[128]{0:T(128)S(1)}, f32[128]{0:T(128)S(1)}, u32[]{:S(2)}, u32[]{:S(2)}) collective-permute-start(f32[128]{0:T(128)S(1)} %multiply_add_fusion.1), channel_id=1, source_target_pairs={{0,28},{4,0},{8,4},{12,8},{16,12},{20,16},{24,20},{28,24},{1,29},{... | collective-permute-start | bytes 1544 | tf_op jit(solution)/shard_map/ppermute | solution.py:11
  89.8 3.9 %collective-permute-start.9 = (f32[128]{0:T(128)S(1)}, f32[128]{0:T(128)S(1)}, u32[]{:S(2)}, u32[]{:S(2)}) collective-permute-start(f32[128]{0:T(128)S(1)} %log_add_fusion.1), channel_id=1, source_target_pairs={{0,4},{4,8},{8,12},{12,16},{16,20},{20,24},{24,28},{28,0},{1,5},{5... | collective-permute-start | bytes 1544 | tf_op jit(solution)/shard_map/ppermute | solution.py:11
  93.7 3.9 %collective-permute-start.10 = (f32[128]{0:T(128)S(1)}, f32[128]{0:T(128)S(1)}, u32[]{:S(2)}, u32[]{:S(2)}) collective-permute-start(f32[128]{0:T(128)S(1)} %collective-permute-done.9), channel_id=1, source_target_pairs={{0,4},{4,8},{8,12},{12,16},{16,20},{20,24},{24,28},{28,0},{1,5},{5... | collective-permute-start | bytes 1544 | tf_op jit(solution)/shard_map/ppermute | solution.py:11
  97.6 3.9 %collective-permute-start.11 = (f32[128]{0:T(128)S(1)}, f32[128]{0:T(128)S(1)}, u32[]{:S(2)}, u32[]{:S(2)}) collective-permute-start(f32[128]{0:T(128)S(1)} %collective-permute-done.10), channel_id=1, source_target_pairs={{0,4},{4,8},{8,12},{12,16},{16,20},{20,24},{24,28},{28,0},{1,5},{5... | collective-permute-start | bytes 1544 | tf_op jit(solution)/shard_map/ppermute | solution.py:11
  104.4 29.4 %copy-start.2 = (bf16[128,1024]{1,0:T(8,128)(2,1)S(1)}, bf16[128,1024]{1,0:T(8,128)(2,1)}, u32[]{:S(2)}) copy-start(bf16[128,1024]{1,0:T(8,128)(2,1)} %param.6) | copy-start | bytes 786436
  104.4 9.6 %collective-permute-start.12 = (f32[128,1024]{1,0:T(8,128)S(1)}, f32[128,1024]{1,0:T(8,128)S(1)}, u32[]{:S(2)}, u32[]{:S(2)}) collective-permute-start(f32[128,1024]{1,0:T(8,128)S(1)} %fusion.17), channel_id=1, source_target_pairs={{0,4},{4,8},{8,12},{12,16},{16,20},{20,24},{24,28},{28,0},{1,5},{5... | collective-permute-start | bytes 1572872 | tf_op jit(solution)/shard_map/ppermute | solution.py:11
  114.4 9.6 %collective-permute-start.13 = (f32[128,1024]{1,0:T(8,128)S(1)}, f32[128,1024]{1,0:T(8,128)S(1)}, u32[]{:S(2)}, u32[]{:S(2)}) collective-permute-start(f32[128,1024]{1,0:T(8,128)S(1)} %convolution_add_fusion), channel_id=1, source_target_pairs={{0,4},{4,8},{8,12},{12,16},{16,20},{20,24},{24,28},{28,0},{1,5},{5... | collective-permute-start | bytes 1572872 | tf_op jit(solution)/shard_map/ppermute | solution.py:11
  124.3 9.6 %collective-permute-start.14 = (f32[128,1024]{1,0:T(8,128)S(1)}, f32[128,1024]{1,0:T(8,128)S(1)}, u32[]{:S(2)}, u32[]{:S(2)}) collective-permute-start(f32[128,1024]{1,0:T(8,128)S(1)} %fusion.21), channel_id=1, source_target_pairs={{0,4},{4,8},{8,12},{12,16},{16,20},{20,24},{24,28},{28,0},{1,5},{5... | collective-permute-start | bytes 1572872 | tf_op jit(solution)/shard_map/ppermute | solution.py:11
  133.8 10.7 %copy-start.1 = (bf16[128,1024]{1,0:T(8,128)(2,1)S(1)}, bf16[128,1024]{1,0:T(8,128)(2,1)}, u32[]{:S(2)}) copy-start(bf16[128,1024]{1,0:T(8,128)(2,1)} %param.7) | copy-start | bytes 786436
Sparse Core Ops, SparseCore 0:
  10.2 30.6 all-gather.5
  104.1 40.3 reduce-scatter.1
where the time goes:
time: 155 us
  waiting for transfers between devices  65.7 us (42%)
  blocking collectives  35.8 us (23%)
  starting transfers between devices  17.9 us (12%)
  between operations  14.9 us (10%)
  other arithmetic  10.8 us (7%)
  matrix products  8.74 us (6%)
    ppermute x15, waiting for transfers between devices, passed_along(): lax.ppermute(array, axis, [(i, (i + by) % count) for i in range(count)])  45.1 us
    all_gather x3, blocking collectives, combined_all(): gathered = jax.tree.map(lambda a: lax.all_gather(a, axis), part)  35.8 us
    ppermute x15, starting transfers between devices, passed_along(): lax.ppermute(array, axis, [(i, (i + by) % count) for i in range(count)])  17.8 us
    all_gather x1, waiting for transfers between devices, on_device(): home_tile = lax.all_gather(txt_own, 'rep', axis=0, tiled=True)  11.4 us
    reduce_scatter x1, waiting for transfers between devices, on_device(): lax.psum_scatter(text_terms, 'rep', scatter_dimension=0, tiled=True)  9.15 us
    dot_general x4, matrix products, tile_scores(): jnp.einsum('id,jd->ij', img_part, text_tile, preferred_element_type=jnp.f...  3.59 us
    dot_general x4, matrix products, on_device(): jnp.einsum('ij,id->jd', weight, tile, preferred_element_type=jnp.float32)  3.56 us
  transfers between devices with their start and end apart: 17, of which 10 were waited for; matrix products, arithmetic and copies ran while one was open for 7% of the time, Pallas kernels for 0%

commit v1 on v0

--- a/solution.py
+++ b/solution.py
@@ -4,6 +4,16 @@
 from jax.sharding import PartitionSpec as P
 
 STEPS = 4
+
+
+def pass_along(array, axis, dim):
+    size = lax.axis_size(axis)
+    held, pieces = (array, [array])
+    for _ in range(size - 1):
+        held = lax.ppermute(held, axis, [(i, (i + 1) % size) for i in range(size)])
+        pieces.insert(0, held)
+    flat = jnp.concatenate(pieces, axis=dim)
+    return jnp.roll(flat, (lax.axis_index(axis) + 1) * array.shape[dim], axis=dim)
 
 
 def passed_along(array, axis, by):
@@ -55,7 +65,7 @@
     txt_unit, txt_inverse = normalize(text)
     img_tile = img_unit.astype(jnp.bfloat16)
     txt_own = txt_unit.astype(jnp.bfloat16)
-    home_tile = lax.all_gather(txt_own, "rep", axis=0, tiled=True)
+    home_tile = pass_along(txt_own, "rep", 0)
     block_rows = home_tile.shape[0]
     columns = lax.broadcasted_iota(jnp.int32, (row_count, block_rows), 1)
     onehot = (positive[0][:, None] == columns).astype(jnp.float32)

time: 155 us -> 155 us (level)
  local copies, waits for them, and re-layouts: 0.68 us -> 4.42 us
  starting transfers between devices: 17.9 us -> 14.3 us
  waiting for transfers between devices: 65.7 us -> 62.6 us
    ppermute x0 -> x3, waiting for transfers between devices: none -> 19.3 us  [pass_along(): held = lax.ppermute(held, axis, [(i, (i + 1) % size) for i in range(size)])]
    all_gather x1 -> x0, waiting for transfers between devices: 11.4 us -> none  [on_device(): home_tile = lax.all_gather(txt_own, 'rep', axis=0, tiled=True)]
    ppermute x15, waiting for transfers between devices: 45.1 us -> 36.9 us  [passed_along(): lax.ppermute(array, axis, [(i, (i + by) % count) for i in range(count)])]
    ppermute x15, starting transfers between devices: 17.8 us -> 11.2 us  [passed_along(): lax.ppermute(array, axis, [(i, (i + by) % count) for i in range(count)])]
    unnamed x11 -> x33, local copies, waits for them, and re-layouts: 0.03 us -> 3.77 us
    ppermute x0 -> x3, starting transfers between devices: none -> 3.11 us  [pass_along(): held = lax.ppermute(held, axis, [(i, (i + 1) % size) for i in range(size)])]
    reduce_scatter x1, waiting for transfers between devices: 9.15 us -> 6.36 us  [on_device(): lax.psum_scatter(text_terms, 'rep', scatter_dimension=0, tiled=True)]
    dot_general x4, matrix products: 1.59 us -> 3.39 us  [on_device(): jnp.dot(weight, home_tile, preferred_element_type=jnp.float32)]
  transfers between devices with their start and end apart: 17 -> 19, of which waited for: 10 -> 10; matrix products, arithmetic and copies ran while one was open for 7% -> 11% of each run, Pallas kernels for 0% -> 0%
where the time goes in v1:
time: 155 us; the launch traced here: 154 us
  waiting for transfers between devices  62.6 us (40%)
  blocking collectives  35.8 us (23%)
  between operations  15 us (10%)
  starting transfers between devices  14.3 us (9%)
  other arithmetic  11.5 us (7%)
  matrix products  10.2 us (7%)
  local copies, waits for them, and re-layouts  4.42 us (3%)
    ppermute x15, waiting for transfers between devices, passed_along(): lax.ppermute(array, axis, [(i, (i + by) % count) for i in range(count)])  36.9 us
    all_gather x3, blocking collectives, combined_all(): gathered = jax.tree.map(lambda a: lax.all_gather(a, axis), part)  35.8 us
    ppermute x3, waiting for transfers between devices, pass_along(): held = lax.ppermute(held, axis, [(i, (i + 1) % size) for i in range(size)])  19.3 us
    ppermute x15, starting transfers between devices, passed_along(): lax.ppermute(array, axis, [(i, (i + by) % count) for i in range(count)])  11.2 us
    reduce_scatter x1, waiting for transfers between devices, on_device(): lax.psum_scatter(text_terms, 'rep', scatter_dimension=0, tiled=True)  6.36 us
    dot_general x4, matrix products, on_device(): jnp.einsum('ij,id->jd', weight, tile, preferred_element_type=jnp.float32)  4.56 us
    unnamed x33, local copies, waits for them, and re-layouts  3.77 us
    dot_general x4, matrix products, on_device(): jnp.dot(weight, home_tile, preferred_element_type=jnp.float32)  3.39 us
  transfers between devices with their start and end apart: 19, of which 10 were waited for; matrix products, arithmetic and copies ran while one was open for 11% of the time, Pallas kernels for 0%

profile of v1, /device:TPU:0, one launch (start us, length us, event | category | flops | bytes accessed | tf_op | source)
XLA Modules:
  0.0 154.0 jit_solution(2970192780338975937)
XLA Ops:
  7.2 1.1 fusion.13
  8.3 1.1 fusion.2
  9.4 3.1 %collective-permute-start = (bf16[128,1024]{1,0:T(8,128)(2,1)S(1)}, bf16[128,1024]{1,0:T(8,128)(2,1)S(1)}, u32[]{:S(2)}, u32[]{:S(2)}) collective-permute-start(bf16[128,1024]{1,0:T(8,128)(2,1)S(1)} %fusion.2), channel_id=1, source_target_pairs={{0,1},{1,2},{2,3},{3,0},{4,5},{5,6},{6,7},{7,4},{8,9},{9,10},{10,1... | collective-permute-start | bytes 786440 | tf_op jit(solution)/shard_map/ppermute | solution.py:13
  12.5 1.1 fusion.9
  13.6 1.1 fusion.5
  14.7 1.7 %collective-permute-start.4 = (bf16[128,1024]{1,0:T(8,128)(2,1)S(1)}, bf16[128,1024]{1,0:T(8,128)(2,1)S(1)}, u32[]{:S(2)}, u32[]{:S(2)}) collective-permute-start(bf16[128,1024]{1,0:T(8,128)(2,1)S(1)} %fusion.5), channel_id=1, source_target_pairs={{0,28},{4,0},{8,4},{12,8},{16,12},{20,16},{24,20},{28,24},{1,29},{... | collective-permute-start | bytes 786440 | tf_op jit(solution)/shard_map/ppermute | solution.py:21
  16.4 4.5 %collective-permute-done = bf16[128,1024]{1,0:T(8,128)(2,1)S(1)} collective-permute-done((bf16[128,1024]{1,0:T(8,128)(2,1)S(1)}, bf16[128,1024]{1,0:T(8,128)(2,1)S(1)}, u32[]{:S(2)}, u32[]{:S(2)}) %collective-permute-start) | collective-permute-done | bytes 262176 | tf_op jit(solution)/shard_map/ppermute | solution.py:13
  20.9 2.2 %collective-permute-start.6 = (bf16[128,1024]{1,0:T(8,128)(2,1)S(1)}, bf16[128,1024]{1,0:T(8,128)(2,1)S(1)}, u32[]{:S(2)}, u32[]{:S(2)}) collective-permute-start(bf16[128,1024]{1,0:T(8,128)(2,1)S(1)} %collective-permute-done.4), channel_id=1, source_target_pairs={{0,28},{4,0},{8,4},{12,8},{16,12},{20,16},{24,20},{28,24},{1,29},{... | collective-permute-start | bytes 786440 | tf_op jit(solution)/shard_map/ppermute | solution.py:21
  23.1 7.1 %collective-permute-done.1 = bf16[128,1024]{1,0:T(8,128)(2,1)S(1)} collective-permute-done((bf16[128,1024]{1,0:T(8,128)(2,1)S(1)}, bf16[128,1024]{1,0:T(8,128)(2,1)S(1)}, u32[]{:S(2)}, u32[]{:S(2)}) %collective-permute-start.1) | collective-permute-done | bytes 262176 | tf_op jit(solution)/shard_map/ppermute | solution.py:13
  30.9 7.8 %collective-permute-done.2 = bf16[128,1024]{1,0:T(8,128)(2,1)} collective-permute-done((bf16[128,1024]{1,0:T(8,128)(2,1)S(1)}, bf16[128,1024]{1,0:T(8,128)(2,1)}, u32[]{:S(2)}, u32[]{:S(2)}) %collective-permute-start.2) | collective-permute-done | bytes 262176 | tf_op jit(solution)/shard_map/ppermute | solution.py:13
  38.6 1.0 constant_dynamic-update-slice_fusion.7
  39.7 1.0 constant_dynamic-update-slice_fusion.6
  40.8 1.0 constant_dynamic-update-slice_fusion.3
  42.0 0.6 fusion.44
  42.6 0.2 fusion.15
  42.8 11.9 %all-gather.3 = f32[4,1,512]{2,1,0:T(1,128)S(1)} all-gather(f32[1,1,512]{2,1,0:T(1,128)S(1)} %bitcast.69), channel_id=2, replica_groups=mesh['blk'=8,'rep'=4] {'rep'}, dimensions={0}, use_global_device_ids=true | all-gather | bytes 10240 | tf_op jit(solution)/shard_map/all_gather | solution.py:25
  54.8 2.1 %collective-permute-start.9 = (f32[128]{0:T(128)S(1)}, f32[128]{0:T(128)S(1)}, u32[]{:S(2)}, u32[]{:S(2)}) collective-permute-start(f32[128]{0:T(128)S(1)} %get-tuple-element.188), channel_id=1, source_target_pairs={{0,28},{4,0},{8,4},{12,8},{16,12},{20,16},{24,20},{28,24},{1,29},{... | collective-permute-start | bytes 1544 | tf_op jit(solution)/shard_map/ppermute | solution.py:21
  56.9 0.6 fusion.43
  57.5 0.6 fusion.45
  58.1 0.7 copy-done.7
  58.8 0.6 fusion.46
  59.7 1.1 collective-permute-start.10
  60.8 2.6 %collective-permute-start.7 = (f32[128]{0:T(128)S(1)}, f32[128]{0:T(128)S(1)}, u32[]{:S(2)}, u32[]{:S(2)}) collective-permute-start(f32[128]{0:T(128)S(1)} %max.62), channel_id=1, source_target_pairs={{0,28},{4,0},{8,4},{12,8},{16,12},{20,16},{24,20},{28,24},{1,29},{... | collective-permute-start | bytes 1544 | tf_op jit(solution)/shard_map/ppermute | solution.py:21
  63.6 1.1 collective-permute-start.11
  64.7 0.2 exponential_reduce_fusion
  64.9 11.9 %all-gather.2 = f32[4,1,512]{2,1,0:T(1,128)S(1)} all-gather(f32[1,1,512]{2,1,0:T(1,128)S(1)} %get-tuple-element.223), channel_id=1, replica_groups=mesh['blk'=8,'rep'=4] {'rep'}, dimensions={0}, use_global_device_ids=true | all-gather | bytes 10240 | tf_op jit(solution)/shard_map/all_gather | solution.py:25
  76.9 11.9 %all-gather.1 = f32[4,1,512]{2,1,0:T(1,128)S(1)} all-gather(f32[1,1,512]{2,1,0:T(1,128)S(1)} %get-tuple-element.224), channel_id=1, replica_groups=mesh['blk'=8,'rep'=4] {'rep'}, dimensions={0}, use_global_device_ids=true | all-gather | bytes 10240 | tf_op jit(solution)/shard_map/all_gather | solution.py:25
  88.8 0.3 while.19
  89.2 3.9 %collective-permute-done.12 = f32[128]{0:T(128)S(1)} collective-permute-done((f32[128]{0:T(128)S(1)}, f32[128]{0:T(128)S(1)}, u32[]{:S(2)}, u32[]{:S(2)}) %collective-permute-start.12) | collective-permute-done | bytes 544 | tf_op jit(solution)/shard_map/ppermute | solution.py:21
  93.1 1.5 fusion.40
  94.6 2.3 %collective-permute-done.13 = f32[128]{0:T(128)S(1)} collective-permute-done((f32[128]{0:T(128)S(1)}, f32[128]{0:T(128)S(1)}, u32[]{:S(2)}, u32[]{:S(2)}) %collective-permute-start.13) | collective-permute-done | bytes 544 | tf_op jit(solution)/shard_map/ppermute | solution.py:21
  97.0 0.5 fusion.41
  97.5 3.3 %collective-permute-done.14 = f32[128]{0:T(128)S(1)} collective-permute-done((f32[128]{0:T(128)S(1)}, f32[128]{0:T(128)S(1)}, u32[]{:S(2)}, u32[]{:S(2)}) %collective-permute-start.14) | collective-permute-done | bytes 544 | tf_op jit(solution)/shard_map/ppermute | solution.py:21
  100.8 0.6 fusion.42
  101.4 1.9 %add_add_fusion = f32[512,1024]{1,0:T(8,128)} fusion(f32[512,1024]{1,0:T(8,128)S(1)} %fusion.42, f32[512,1024]{1,0:T(8,128)S(1)} %fusion.41, f32[512,1024]{1,0:T(8,128)S(1)} %fusion.40, bf16[128,1024]{1,0:T(8,128)(2,1)S(1)} %copy-done.8, f32[128,512]{1,0:T(8,128)S(1)} %get-tuple-element.228, f32[512]{0:T(512)S(1)} %get-tuple-element.220, ...), kind=kOutput, calls=%fused_computation.4 | convolution fusion | flops 136118272 | bytes 8915456 | tf_op jit(solution)/shard_map/ij,id->jd/dot_general | solution.py:113
  103.4 0.4 fusion.23
  103.8 0.4 fusion.21
  104.2 9.1 %collective-permute-done.15 = f32[128,1024]{1,0:T(8,128)S(1)} collective-permute-done((f32[128,1024]{1,0:T(8,128)S(1)}, f32[128,1024]{1,0:T(8,128)S(1)}, u32[]{:S(2)}, u32[]{:S(2)}) %collective-permute-start.15) | collective-permute-done | bytes 524320 | tf_op jit(solution)/shard_map/ppermute | solution.py:21
  113.4 9.5 %collective-permute-done.16 = f32[128,1024]{1,0:T(8,128)S(1)} collective-permute-done((f32[128,1024]{1,0:T(8,128)S(1)}, f32[128,1024]{1,0:T(8,128)S(1)}, u32[]{:S(2)}, u32[]{:S(2)}) %collective-permute-start.16) | collective-permute-done | bytes 524320 | tf_op jit(solution)/shard_map/ppermute | solution.py:21
  122.9 1.2 fusion.29
  124.1 0.6 dynamic_slice.51
  124.7 0.5 sub.242
  125.2 8.7 %collective-permute-done.17 = f32[128,1024]{1,0:T(8,128)} collective-permute-done((f32[128,1024]{1,0:T(8,128)}, f32[128,1024]{1,0:T(8,128)}, u32[]{:S(2)}, u32[]{:S(2)}) %collective-permute-start.17) | collective-permute-done | bytes 524320 | tf_op jit(solution)/shard_map/ppermute | solution.py:21
  133.9 1.5 fusion.6
  135.4 2.1 %fusion.8 = f32[128,1024]{1,0:T(8,128)} fusion(bf16[128,1024]{1,0:T(8,128)(2,1)S(1)} %copy-done.1, f32[128]{0:T(128)S(1)} %get-tuple-element.229, f32[128]{0:T(128)S(1)} %add_rsqrt_fusion.1, f32[128,1024]{1,0:T(8,128)} %collective-permute-done.17, f32[128,1024]{1,0:T(8,128)S(1)} %get-tuple-element.230, f32[]{:T(128)} %bitcast.48), kind=kLoop, calls=%fused_computation.21 | loop fusion | flops 917504 | bytes 1836036 | tf_op jit(solution)/shard_map/mul | solution.py:122
  137.5 6.4 %reduce-scatter.2.cloned.1.call-done = f32[128,1024]{1,0:T(8,128)} async-done(((f32[512,1024]{1,0:T(8,128)}), f32[128,1024]{1,0:T(8,128)}) %reduce-scatter.2.cloned.1.call-update) | async-done | bytes 524304 | tf_op jit(solution)/shard_map/reduce_scatter | solution.py:119
  143.8 1.3 fusion.10
  145.1 2.1 %fusion.12 = f32[128,1024]{1,0:T(8,128)} fusion(bf16[128,1024]{1,0:T(8,128)(2,1)S(1)} %copy-done, f32[128,1024]{1,0:T(8,128)} %reduce-scatter.2.cloned.1.call-done, f32[128]{0:T(128)S(1)} %fusion.10, f32[]{:T(128)} %bitcast.46, f32[128]{0:T(128)S(1)} %add_rsqrt_fusion), kind=kLoop, calls=%fused_computation.25 | loop fusion | flops 786432 | bytes 1311748 | tf_op jit(solution)/shard_map/mul | solution.py:125
  (81 shorter events, 1.5 us)
Async XLA Ops:
  7.2 33.5 %copy-start = (bf16[128,1024]{1,0:T(8,128)(2,1)S(1)}, bf16[128,1024]{1,0:T(8,128)(2,1)}, u32[]{:S(2)}) copy-start(bf16[128,1024]{1,0:T(8,128)(2,1)} %param.7) | copy-start | bytes 786436
  7.2 136.7 %reduce-scatter.2.cloned.1.call-start = ((), (), s32[]{:S(2)}) async-start(), calls=%async_computation.1 | async-start | bytes 2621440 | tf_op jit(solution)/shard_map/reduce_scatter | solution.py:119
  9.4 11.4 %collective-permute-start = (bf16[128,1024]{1,0:T(8,128)(2,1)S(1)}, bf16[128,1024]{1,0:T(8,128)(2,1)S(1)}, u32[]{:S(2)}, u32[]{:S(2)}) collective-permute-start(bf16[128,1024]{1,0:T(8,128)(2,1)S(1)} %fusion.2), channel_id=1, source_target_pairs={{0,1},{1,2},{2,3},{3,0},{4,5},{5,6},{6,7},{7,4},{8,9},{9,10},{10,1... | collective-permute-start | bytes 786440 | tf_op jit(solution)/shard_map/ppermute | solution.py:13
  14.7 27.3 %copy-start.2 = (bf16[128,1024]{1,0:T(8,128)(2,1)}, bf16[128,1024]{1,0:T(8,128)(2,1)S(1)}, u32[]{:S(2)}) copy-start(bf16[128,1024]{1,0:T(8,128)(2,1)S(1)} %fusion.5) | copy-start | bytes 786436
  14.7 6.2 %collective-permute-start.4 = (bf16[128,1024]{1,0:T(8,128)(2,1)S(1)}, bf16[128,1024]{1,0:T(8,128)(2,1)S(1)}, u32[]{:S(2)}, u32[]{:S(2)}) collective-permute-start(bf16[128,1024]{1,0:T(8,128)(2,1)S(1)} %fusion.5), channel_id=1, source_target_pairs={{0,28},{4,0},{8,4},{12,8},{16,12},{20,16},{24,20},{28,24},{1,29},{... | collective-permute-start | bytes 786440 | tf_op jit(solution)/shard_map/ppermute | solution.py:21
  20.9 9.3 %collective-permute-start.1 = (bf16[128,1024]{1,0:T(8,128)(2,1)S(1)}, bf16[128,1024]{1,0:T(8,128)(2,1)S(1)}, u32[]{:S(2)}, u32[]{:S(2)}) collective-permute-start(bf16[128,1024]{1,0:T(8,128)(2,1)S(1)} %collective-permute-done), channel_id=1, source_target_pairs={{0,1},{1,2},{2,3},{3,0},{4,5},{5,6},{6,7},{7,4},{8,9},{9,10},{10,1... | collective-permute-start | bytes 786440 | tf_op jit(solution)/shard_map/ppermute | solution.py:13
  20.9 36.0 %copy-start.4 = (bf16[128,1024]{1,0:T(8,128)(2,1)}, bf16[128,1024]{1,0:T(8,128)(2,1)S(1)}, u32[]{:S(2)}) copy-start(bf16[128,1024]{1,0:T(8,128)(2,1)S(1)} %collective-permute-done.4) | copy-start | bytes 786436
  20.9 9.9 %collective-permute-start.6 = (bf16[128,1024]{1,0:T(8,128)(2,1)S(1)}, bf16[128,1024]{1,0:T(8,128)(2,1)S(1)}, u32[]{:S(2)}, u32[]{:S(2)}) collective-permute-start(bf16[128,1024]{1,0:T(8,128)(2,1)S(1)} %collective-permute-done.4), channel_id=1, source_target_pairs={{0,28},{4,0},{8,4},{12,8},{16,12},{20,16},{24,20},{28,24},{1,29},{... | collective-permute-start | bytes 786440 | tf_op jit(solution)/shard_map/ppermute | solution.py:21
  30.1 0.8 copy-start.9
  30.1 8.5 %collective-permute-start.2 = (bf16[128,1024]{1,0:T(8,128)(2,1)S(1)}, bf16[128,1024]{1,0:T(8,128)(2,1)}, u32[]{:S(2)}, u32[]{:S(2)}) collective-permute-start(bf16[128,1024]{1,0:T(8,128)(2,1)S(1)} %collective-permute-done.1), channel_id=1, source_target_pairs={{0,1},{1,2},{2,3},{3,0},{4,5},{5,6},{6,7},{7,4},{8,9},{9,10},{10,1... | collective-permute-start | bytes 786440 | tf_op jit(solution)/shard_map/ppermute | solution.py:13
  30.8 26.7 %copy-start.6 = (bf16[128,1024]{1,0:T(8,128)(2,1)}, bf16[128,1024]{1,0:T(8,128)(2,1)S(1)}, u32[]{:S(2)}) copy-start(bf16[128,1024]{1,0:T(8,128)(2,1)S(1)} %collective-permute-done.6) | copy-start | bytes 786436
  30.8 27.2 %collective-permute-start.8 = (bf16[128,1024]{1,0:T(8,128)(2,1)S(1)}, bf16[128,1024]{1,0:T(8,128)(2,1)S(1)}, u32[]{:S(2)}, u32[]{:S(2)}) collective-permute-start(bf16[128,1024]{1,0:T(8,128)(2,1)S(1)} %collective-permute-done.6), channel_id=1, source_target_pairs={{0,28},{4,0},{8,4},{12,8},{16,12},{20,16},{24,20},{28,24},{1,29},{... | collective-permute-start | bytes 786440 | tf_op jit(solution)/shard_map/ppermute | solution.py:21
  38.6 3.1 %copy-start.10 = (bf16[128,1024]{1,0:T(8,128)(2,1)S(1)}, bf16[128,1024]{1,0:T(8,128)(2,1)}, u32[]{:S(2)}) copy-start(bf16[128,1024]{1,0:T(8,128)(2,1)} %copy-done.9) | copy-start | bytes 786436
  40.7 1.9 %copy-start.11 = (s32[1,128]{1,0:T(1,128)S(1)}, s32[1,128]{1,0:T(1,128)}, u32[]{:S(2)}) copy-start(s32[1,128]{1,0:T(1,128)} %param.8) | copy-start | bytes 1540
  54.7 4.6 %collective-permute-start.3 = (f32[128]{0:T(128)S(1)}, f32[128]{0:T(128)S(1)}, u32[]{:S(2)}, u32[]{:S(2)}) collective-permute-start(f32[128]{0:T(128)S(1)} %get-tuple-element.198), channel_id=1, source_target_pairs={{0,28},{4,0},{8,4},{12,8},{16,12},{20,16},{24,20},{28,24},{1,29},{... | collective-permute-start | bytes 1544 | tf_op jit(solution)/shard_map/ppermute | solution.py:21
  54.8 4.9 %collective-permute-start.9 = (f32[128]{0:T(128)S(1)}, f32[128]{0:T(128)S(1)}, u32[]{:S(2)}, u32[]{:S(2)}) collective-permute-start(f32[128]{0:T(128)S(1)} %get-tuple-element.188), channel_id=1, source_target_pairs={{0,28},{4,0},{8,4},{12,8},{16,12},{20,16},{24,20},{28,24},{1,29},{... | collective-permute-start | bytes 1544 | tf_op jit(solution)/shard_map/ppermute | solution.py:21
  58.0 0.7 copy-start.7
  59.3 1.4 collective-permute-start.5
  59.7 3.9 %collective-permute-start.10 = (f32[128]{0:T(128)S(1)}, f32[128]{0:T(128)S(1)}, u32[]{:S(2)}, u32[]{:S(2)}) collective-permute-start(f32[128]{0:T(128)S(1)} %multiply_add_fusion.2), channel_id=1, source_target_pairs={{0,28},{4,0},{8,4},{12,8},{16,12},{20,16},{24,20},{28,24},{1,29},{... | collective-permute-start | bytes 1544 | tf_op jit(solution)/shard_map/ppermute | solution.py:21
  60.8 3.9 %collective-permute-start.7 = (f32[128]{0:T(128)S(1)}, f32[128]{0:T(128)S(1)}, u32[]{:S(2)}, u32[]{:S(2)}) collective-permute-start(f32[128]{0:T(128)S(1)} %max.62), channel_id=1, source_target_pairs={{0,28},{4,0},{8,4},{12,8},{16,12},{20,16},{24,20},{28,24},{1,29},{... | collective-permute-start | bytes 1544 | tf_op jit(solution)/shard_map/ppermute | solution.py:21
  63.6 25.5 %collective-permute-start.11 = (f32[128]{0:T(128)S(1)}, f32[128]{0:T(128)S(1)}, u32[]{:S(2)}, u32[]{:S(2)}) collective-permute-start(f32[128]{0:T(128)S(1)} %multiply_add_fusion.1), channel_id=1, source_target_pairs={{0,28},{4,0},{8,4},{12,8},{16,12},{20,16},{24,20},{28,24},{1,29},{... | collective-permute-start | bytes 1544 | tf_op jit(solution)/shard_map/ppermute | solution.py:21
  89.1 7.9 %copy-start.5 = (bf16[128,1024]{1,0:T(8,128)(2,1)S(1)}, bf16[128,1024]{1,0:T(8,128)(2,1)}, u32[]{:S(2)}) copy-start(bf16[128,1024]{1,0:T(8,128)(2,1)} %copy-done.4) | copy-start | bytes 786436
  89.1 3.9 %collective-permute-start.12 = (f32[128]{0:T(128)S(1)}, f32[128]{0:T(128)S(1)}, u32[]{:S(2)}, u32[]{:S(2)}) collective-permute-start(f32[128]{0:T(128)S(1)} %log_add_fusion.1), channel_id=1, source_target_pairs={{0,4},{4,8},{8,12},{12,16},{16,20},{20,24},{24,28},{28,0},{1,5},{5... | collective-permute-start | bytes 1544 | tf_op jit(solution)/shard_map/ppermute | solution.py:21
  93.1 3.9 %collective-permute-start.13 = (f32[128]{0:T(128)S(1)}, f32[128]{0:T(128)S(1)}, u32[]{:S(2)}, u32[]{:S(2)}) collective-permute-start(f32[128]{0:T(128)S(1)} %collective-permute-done.12), channel_id=1, source_target_pairs={{0,4},{4,8},{8,12},{12,16},{16,20},{20,24},{24,28},{28,0},{1,5},{5... | collective-permute-start | bytes 1544 | tf_op jit(solution)/shard_map/ppermute | solution.py:21
  93.1 7.8 %copy-start.3 = (bf16[128,1024]{1,0:T(8,128)(2,1)S(1)}, bf16[128,1024]{1,0:T(8,128)(2,1)}, u32[]{:S(2)}) copy-start(bf16[128,1024]{1,0:T(8,128)(2,1)} %copy-done.2) | copy-start | bytes 786436
  94.6 6.8 %copy-start.8 = (bf16[128,1024]{1,0:T(8,128)(2,1)S(1)}, bf16[128,1024]{1,0:T(8,128)(2,1)}, u32[]{:S(2)}) copy-start(bf16[128,1024]{1,0:T(8,128)(2,1)} %copy-done.7) | copy-start | bytes 786436
  96.9 3.9 %collective-permute-start.14 = (f32[128]{0:T(128)S(1)}, f32[128]{0:T(128)S(1)}, u32[]{:S(2)}, u32[]{:S(2)}) collective-permute-start(f32[128]{0:T(128)S(1)} %collective-permute-done.13), channel_id=1, source_target_pairs={{0,4},{4,8},{8,12},{12,16},{16,20},{20,24},{24,28},{28,0},{1,5},{5... | collective-permute-start | bytes 1544 | tf_op jit(solution)/shard_map/ppermute | solution.py:21
  103.7 9.6 %collective-permute-start.15 = (f32[128,1024]{1,0:T(8,128)S(1)}, f32[128,1024]{1,0:T(8,128)S(1)}, u32[]{:S(2)}, u32[]{:S(2)}) collective-permute-start(f32[128,1024]{1,0:T(8,128)S(1)} %fusion.23), channel_id=1, source_target_pairs={{0,4},{4,8},{8,12},{12,16},{16,20},{20,24},{24,28},{28,0},{1,5},{5... | collective-permute-start | bytes 1572872 | tf_op jit(solution)/shard_map/ppermute | solution.py:21
  104.2 29.7 %copy-start.1 = (bf16[128,1024]{1,0:T(8,128)(2,1)S(1)}, bf16[128,1024]{1,0:T(8,128)(2,1)}, u32[]{:S(2)}) copy-start(bf16[128,1024]{1,0:T(8,128)(2,1)} %param.6) | copy-start | bytes 786436
  113.4 9.6 %collective-permute-start.16 = (f32[128,1024]{1,0:T(8,128)S(1)}, f32[128,1024]{1,0:T(8,128)S(1)}, u32[]{:S(2)}, u32[]{:S(2)}) collective-permute-start(f32[128,1024]{1,0:T(8,128)S(1)} %add.184), channel_id=1, source_target_pairs={{0,4},{4,8},{8,12},{12,16},{16,20},{20,24},{24,28},{28,0},{1,5},{5... | collective-permute-start | bytes 1572872 | tf_op jit(solution)/shard_map/ppermute | solution.py:21
  124.1 9.8 %collective-permute-start.17 = (f32[128,1024]{1,0:T(8,128)}, f32[128,1024]{1,0:T(8,128)}, u32[]{:S(2)}, u32[]{:S(2)}) collective-permute-start(f32[128,1024]{1,0:T(8,128)} %fusion.29), channel_id=1, source_target_pairs={{0,4},{4,8},{8,12},{12,16},{16,20},{20,24},{24,28},{28,0},{1,5},{5... | collective-permute-start | bytes 1572872 | tf_op jit(solution)/shard_map/ppermute | solution.py:21
Sparse Core Ops, SparseCore 0:
  103.5 40.3 reduce-scatter.1
